TPU v7x, 256 devices: a whole 4x4x8 slice. The times are simulated.
256 devices in a mesh: seq: 16 (over y_hi, z), head: 16 (over y_lo, x, core).
Axes of the slice: x: 4, y: 4 (y_hi: 2, y_lo: 2; y = y_hi * 2 + y_lo), z: 8, core: 2. Of those that a mesh axis runs over, the one named last changes fastest.
Arguments:
- queries: bfloat16 [16384, 4096], P(('seq', 'head')), may hold values from -9 to 9, as said below
- keys: bfloat16 [16384, 512], P(('seq', 'head')), may hold values from -9 to 9, as said below
- values: bfloat16 [16384, 512], P(('seq', 'head')), may hold values from -6 to 6
Outputs:
- attended: bfloat16 [16384, 4096], P(('seq', 'head'))
Inputs may be any that keep to these rules, and one draw needn't show every extreme that they name: `queries`: query entries are of order one except on a few rows. `keys`: key entries are of order one except on a few rows.
All inputs are finite; a program needn't handle non-finite values.
Results may differ from a plain program's by a relative error of at most 0.005.
Values may be sent and summed in bfloat16 or wider, within the bound.
A program may use at most 64 MiB of HBM per device.

v0:
```python
import math

import jax
import jax.numpy as jnp
from jax import lax
from jax.sharding import PartitionSpec as P

H = 32
KV = 4
DH = 128


def sent_together(arrays, axis, split_dim, concat_dim, along):
    both = jnp.concatenate(arrays, axis=along)
    out, at, gathered = (
        lax.all_to_all(both, axis, split_axis=split_dim, concat_axis=concat_dim, tiled=True),
        0,
        [],
    )
    for a in arrays:
        gathered.append(lax.slice_in_dim(out, at, at + a.shape[along], axis=along))
        at += a.shape[along]
    return tuple(gathered)


def in_one_piece(arrays, axis, dim, along):
    ends, at = ([], 0)
    for a in arrays[:-1]:
        at += a.shape[along]
        ends.append(at)
    both = jnp.concatenate(arrays, axis=along)
    return tuple(jnp.split(lax.all_gather(both, axis, axis=dim, tiled=True), ends, axis=along))


def per_device(queries, keys, values):
    n_head = lax.axis_size("head")
    tok = queries.shape[0]
    per_dev = H // n_head
    group = tok * n_head
    scale = 1.0 / math.sqrt(DH)
    me_seq = lax.axis_index("seq")
    arranged = queries.reshape(tok, n_head, per_dev * DH)
    received = lax.all_to_all(arranged, "head", split_axis=1, concat_axis=0, tiled=True)
    mine = received.reshape(group, per_dev, DH)
    first = me_seq * group
    last = first + group - 1
    query_pos = first + jnp.arange(group, dtype=jnp.int32)
    init = (
        jnp.full((group, per_dev), -1e30, jnp.float32),
        jnp.zeros((group, per_dev), jnp.float32),
        jnp.zeros((group, per_dev, DH), jnp.float32),
    )
    wide_keys = jnp.repeat(keys.reshape(tok, KV, DH), n_head // KV, axis=1)
    wide_values = jnp.repeat(values.reshape(tok, KV, DH), n_head // KV, axis=1)
    slot_keys, slot_values = sent_together((wide_keys, wide_values), "head", 1, 0, 2)
    k_piece, v_piece = in_one_piece(
        (slot_keys.reshape(group, DH), slot_values.reshape(group, DH)), "seq", 0, 1
    )
    rows = k_piece.shape[0]
    width = math.gcd(rows, 512)

    def step(index, state):
        block_start = index * width

        def work(inner):
            running, total, acc = inner
            k_blk = lax.dynamic_slice_in_dim(k_piece, index * width, width, 0)
            v_blk = lax.dynamic_slice_in_dim(v_piece, index * width, width, 0)
            scores = (
                jnp.einsum("ghd,kd->ghk", mine, k_blk, preferred_element_type=jnp.float32) * scale
            )
            key_pos = block_start + jnp.arange(width, dtype=jnp.int32)
            scores = jnp.where(key_pos[None, None, :] <= query_pos[:, None, None], scores, -jnp.inf)
            newmax = jnp.maximum(running, jnp.max(scores, axis=2))
            factor = jnp.exp(running - newmax)
            expo = jnp.exp(scores - newmax[:, :, None])
            total = factor * total + jnp.sum(expo, axis=2)
            acc = factor[:, :, None] * acc + jnp.einsum(
                "ghk,kd->ghd", expo.astype(jnp.bfloat16), v_blk, preferred_element_type=jnp.float32
            )
            return (newmax, total, acc)

        def skip(inner):
            return inner

        return lax.cond(block_start <= last, work, skip, state)

    state = lax.fori_loop(0, rows // width, step, init)
    running, total, acc = state
    output = (acc / total[:, :, None]).astype(jnp.bfloat16)
    output = output.reshape(group, 1, per_dev * DH)
    returned = lax.all_to_all(output, "head", split_axis=0, concat_axis=1, tiled=True)
    return returned.reshape(tok, H * DH)


def solution(mesh):
    in_specs = (P(("seq", "head"), None), P(("seq", "head"), None), P(("seq", "head"), None))
    out_specs = P(("seq", "head"), None)
    return jax.shard_map(
        per_device, mesh=mesh, in_specs=in_specs, out_specs=out_specs, check_vma=False
    )
```

profile of v0, /device:TPU:249, one launch (start us, length us, event | category | flops | bytes accessed | tf_op | source)
XLA Modules:
  0.0 370.8 jit_solution(2027929912049905887)
XLA Ops:
  8.4 15.3 %all_to_all.48 = bf16[64,16,256]{2,0,1:T(8,128)(2,1)S(1)} all-to-all(bf16[64,16,256]{2,0,1:T(8,128)(2,1)S(1)} %pad_maximum_fusion), channel_id=1, replica_groups=mesh['seq'=16,'head'=16] {'head'}, dimensions={1} | all-to-all | bytes 1048576 | tf_op jit(solution)/shard_map/all_to_all | solution.py:16
  25.5 4.9 %all-to-all-start.1 = ((bf16[64,16,256]{2,0,1:T(8,128)(2,1)}), bf16[64,16,256]{2,0,1:T(8,128)(2,1)S(1)}, u32[]{:S(2)}, u32[]{:S(2)}) async-start(bf16[64,16,256]{2,0,1:T(8,128)(2,1)} %bitcast.61), calls=%async_computation.1 | async-start | bytes 1048576 | tf_op jit(solution)/shard_map/all_to_all | solution.py:43
  30.4 9.5 %all-to-all-done.1 = bf16[64,16,256]{2,0,1:T(8,128)(2,1)S(1)} async-done(((bf16[64,16,256]{2,0,1:T(8,128)(2,1)}), bf16[64,16,256]{2,0,1:T(8,128)(2,1)S(1)}, u32[]{:S(2)}, u32[]{:S(2)}) %all-to-all-start.1) | async-done | bytes 524320 | tf_op jit(solution)/shard_map/all_to_all | solution.py:43
  40.2 113.7 %all-gather.2.cloned.1.call-done = bf16[16384,256]{1,0:T(8,128)(2,1)} async-done(((bf16[1024,256]{1,0:T(8,128)(2,1)}), bf16[16384,256]{1,0:T(8,128)(2,1)}) %all-gather.2.cloned.1.call-update) | async-done | bytes 8388624 | tf_op jit(solution)/shard_map/all_gather | solution.py:32
  153.9 5.7 %fusion.20 = (bf16[16384,128]{1,0:T(8,128)(2,1)}, bf16[16384,128]{1,0:T(8,128)(2,1)}) fusion(bf16[16384,256]{1,0:T(8,128)(2,1)} %all-gather.2.cloned.1.call-done), kind=kLoop, calls=%fused_computation.31 | loop fusion | bytes 16777216 | tf_op jit(solution)/shard_map/split | solution.py:32
  159.7 184.6 %while.18 = (s32[]{:T(128)}, f32[1024,2]{0,1:T(2,128)S(1)}, f32[1024,2]{0,1:T(2,128)S(1)}, f32[1024,2,128]{2,0,1:T(8,128)S(1)}, s32[]{:T(128)}, /*index=5*/bf16[...) while((s32[]{:T(128)}, f32[1024,2]{0,1:T(2,128)S(1)}, ...), condition=%wide.region_5.6_spmd.clone, body=%wide.region_0.5_spmd.clone.sunk | while | flops 549459456 | bytes 17715532 | solution.py:88
  159.7 5.7 %conditional.3 = ((f32[1024,2]{0,1:T(2,128)S(1)}, f32[1024,2]{0,1:T(2,128)S(1)}, f32[1024,2,128]{2,0,1:T(8,128)S(1)})) conditional(s32[]{:T(128)} %convert_element_type.21, (f32[1024,2]{0,1:T(2,128)S(1)}, f32[1024,2]{0,1:T(2,128)S(1)}, f32[1024,2,128]{2,0,1:T(8,128)S(1)}) %tuple.49, (s32[]{:T(128)}, s32[]{:T(128)}, s32[]{:T(128)}, ...), branch_computations={%region_1.0_spmd, %region_2.4_spmd} | conditional | flops 549459456 | bytes 17711198 | solution.py:86
  165.4 5.7 %conditional.3 = ((f32[1024,2]{0,1:T(2,128)S(1)}, f32[1024,2]{0,1:T(2,128)S(1)}, f32[1024,2,128]{2,0,1:T(8,128)S(1)})) conditional(s32[]{:T(128)} %convert_element_type.21, (f32[1024,2]{0,1:T(2,128)S(1)}, f32[1024,2]{0,1:T(2,128)S(1)}, f32[1024,2,128]{2,0,1:T(8,128)S(1)}) %tuple.49, (s32[]{:T(128)}, s32[]{:T(128)}, s32[]{:T(128)}, ...), branch_computations={%region_1.0_spmd, %region_2.4_spmd} | conditional | flops 549459456 | bytes 17711198 | solution.py:86
  171.2 5.7 %conditional.3 = ((f32[1024,2]{0,1:T(2,128)S(1)}, f32[1024,2]{0,1:T(2,128)S(1)}, f32[1024,2,128]{2,0,1:T(8,128)S(1)})) conditional(s32[]{:T(128)} %convert_element_type.21, (f32[1024,2]{0,1:T(2,128)S(1)}, f32[1024,2]{0,1:T(2,128)S(1)}, f32[1024,2,128]{2,0,1:T(8,128)S(1)}) %tuple.49, (s32[]{:T(128)}, s32[]{:T(128)}, s32[]{:T(128)}, ...), branch_computations={%region_1.0_spmd, %region_2.4_spmd} | conditional | flops 549459456 | bytes 17711198 | solution.py:86
  177.0 5.7 %conditional.3 = ((f32[1024,2]{0,1:T(2,128)S(1)}, f32[1024,2]{0,1:T(2,128)S(1)}, f32[1024,2,128]{2,0,1:T(8,128)S(1)})) conditional(s32[]{:T(128)} %convert_element_type.21, (f32[1024,2]{0,1:T(2,128)S(1)}, f32[1024,2]{0,1:T(2,128)S(1)}, f32[1024,2,128]{2,0,1:T(8,128)S(1)}) %tuple.49, (s32[]{:T(128)}, s32[]{:T(128)}, s32[]{:T(128)}, ...), branch_computations={%region_1.0_spmd, %region_2.4_spmd} | conditional | flops 549459456 | bytes 17711198 | solution.py:86
  182.8 5.7 %conditional.3 = ((f32[1024,2]{0,1:T(2,128)S(1)}, f32[1024,2]{0,1:T(2,128)S(1)}, f32[1024,2,128]{2,0,1:T(8,128)S(1)})) conditional(s32[]{:T(128)} %convert_element_type.21, (f32[1024,2]{0,1:T(2,128)S(1)}, f32[1024,2]{0,1:T(2,128)S(1)}, f32[1024,2,128]{2,0,1:T(8,128)S(1)}) %tuple.49, (s32[]{:T(128)}, s32[]{:T(128)}, s32[]{:T(128)}, ...), branch_computations={%region_1.0_spmd, %region_2.4_spmd} | conditional | flops 549459456 | bytes 17711198 | solution.py:86
  188.5 5.7 %conditional.3 = ((f32[1024,2]{0,1:T(2,128)S(1)}, f32[1024,2]{0,1:T(2,128)S(1)}, f32[1024,2,128]{2,0,1:T(8,128)S(1)})) conditional(s32[]{:T(128)} %convert_element_type.21, (f32[1024,2]{0,1:T(2,128)S(1)}, f32[1024,2]{0,1:T(2,128)S(1)}, f32[1024,2,128]{2,0,1:T(8,128)S(1)}) %tuple.49, (s32[]{:T(128)}, s32[]{:T(128)}, s32[]{:T(128)}, ...), branch_computations={%region_1.0_spmd, %region_2.4_spmd} | conditional | flops 549459456 | bytes 17711198 | solution.py:86
  194.3 5.7 %conditional.3 = ((f32[1024,2]{0,1:T(2,128)S(1)}, f32[1024,2]{0,1:T(2,128)S(1)}, f32[1024,2,128]{2,0,1:T(8,128)S(1)})) conditional(s32[]{:T(128)} %convert_element_type.21, (f32[1024,2]{0,1:T(2,128)S(1)}, f32[1024,2]{0,1:T(2,128)S(1)}, f32[1024,2,128]{2,0,1:T(8,128)S(1)}) %tuple.49, (s32[]{:T(128)}, s32[]{:T(128)}, s32[]{:T(128)}, ...), branch_computations={%region_1.0_spmd, %region_2.4_spmd} | conditional | flops 549459456 | bytes 17711198 | solution.py:86
  200.1 5.7 %conditional.3 = ((f32[1024,2]{0,1:T(2,128)S(1)}, f32[1024,2]{0,1:T(2,128)S(1)}, f32[1024,2,128]{2,0,1:T(8,128)S(1)})) conditional(s32[]{:T(128)} %convert_element_type.21, (f32[1024,2]{0,1:T(2,128)S(1)}, f32[1024,2]{0,1:T(2,128)S(1)}, f32[1024,2,128]{2,0,1:T(8,128)S(1)}) %tuple.49, (s32[]{:T(128)}, s32[]{:T(128)}, s32[]{:T(128)}, ...), branch_computations={%region_1.0_spmd, %region_2.4_spmd} | conditional | flops 549459456 | bytes 17711198 | solution.py:86
  203.3 2.4 fusion.8
  205.8 5.7 %conditional.3 = ((f32[1024,2]{0,1:T(2,128)S(1)}, f32[1024,2]{0,1:T(2,128)S(1)}, f32[1024,2,128]{2,0,1:T(8,128)S(1)})) conditional(s32[]{:T(128)} %convert_element_type.21, (f32[1024,2]{0,1:T(2,128)S(1)}, f32[1024,2]{0,1:T(2,128)S(1)}, f32[1024,2,128]{2,0,1:T(8,128)S(1)}) %tuple.49, (s32[]{:T(128)}, s32[]{:T(128)}, s32[]{:T(128)}, ...), branch_computations={%region_1.0_spmd, %region_2.4_spmd} | conditional | flops 549459456 | bytes 17711198 | solution.py:86
  209.1 2.4 fusion.8
  211.6 5.7 %conditional.3 = ((f32[1024,2]{0,1:T(2,128)S(1)}, f32[1024,2]{0,1:T(2,128)S(1)}, f32[1024,2,128]{2,0,1:T(8,128)S(1)})) conditional(s32[]{:T(128)} %convert_element_type.21, (f32[1024,2]{0,1:T(2,128)S(1)}, f32[1024,2]{0,1:T(2,128)S(1)}, f32[1024,2,128]{2,0,1:T(8,128)S(1)}) %tuple.49, (s32[]{:T(128)}, s32[]{:T(128)}, s32[]{:T(128)}, ...), branch_computations={%region_1.0_spmd, %region_2.4_spmd} | conditional | flops 549459456 | bytes 17711198 | solution.py:86
  214.9 2.4 fusion.8
  217.4 5.7 %conditional.3 = ((f32[1024,2]{0,1:T(2,128)S(1)}, f32[1024,2]{0,1:T(2,128)S(1)}, f32[1024,2,128]{2,0,1:T(8,128)S(1)})) conditional(s32[]{:T(128)} %convert_element_type.21, (f32[1024,2]{0,1:T(2,128)S(1)}, f32[1024,2]{0,1:T(2,128)S(1)}, f32[1024,2,128]{2,0,1:T(8,128)S(1)}) %tuple.49, (s32[]{:T(128)}, s32[]{:T(128)}, s32[]{:T(128)}, ...), branch_computations={%region_1.0_spmd, %region_2.4_spmd} | conditional | flops 549459456 | bytes 17711198 | solution.py:86
  220.6 2.4 fusion.8
  223.1 5.7 %conditional.3 = ((f32[1024,2]{0,1:T(2,128)S(1)}, f32[1024,2]{0,1:T(2,128)S(1)}, f32[1024,2,128]{2,0,1:T(8,128)S(1)})) conditional(s32[]{:T(128)} %convert_element_type.21, (f32[1024,2]{0,1:T(2,128)S(1)}, f32[1024,2]{0,1:T(2,128)S(1)}, f32[1024,2,128]{2,0,1:T(8,128)S(1)}) %tuple.49, (s32[]{:T(128)}, s32[]{:T(128)}, s32[]{:T(128)}, ...), branch_computations={%region_1.0_spmd, %region_2.4_spmd} | conditional | flops 549459456 | bytes 17711198 | solution.py:86
  226.4 2.4 fusion.8
  228.9 5.7 %conditional.3 = ((f32[1024,2]{0,1:T(2,128)S(1)}, f32[1024,2]{0,1:T(2,128)S(1)}, f32[1024,2,128]{2,0,1:T(8,128)S(1)})) conditional(s32[]{:T(128)} %convert_element_type.21, (f32[1024,2]{0,1:T(2,128)S(1)}, f32[1024,2]{0,1:T(2,128)S(1)}, f32[1024,2,128]{2,0,1:T(8,128)S(1)}) %tuple.49, (s32[]{:T(128)}, s32[]{:T(128)}, s32[]{:T(128)}, ...), branch_computations={%region_1.0_spmd, %region_2.4_spmd} | conditional | flops 549459456 | bytes 17711198 | solution.py:86
  232.2 2.4 fusion.8
  234.7 5.7 %conditional.3 = ((f32[1024,2]{0,1:T(2,128)S(1)}, f32[1024,2]{0,1:T(2,128)S(1)}, f32[1024,2,128]{2,0,1:T(8,128)S(1)})) conditional(s32[]{:T(128)} %convert_element_type.21, (f32[1024,2]{0,1:T(2,128)S(1)}, f32[1024,2]{0,1:T(2,128)S(1)}, f32[1024,2,128]{2,0,1:T(8,128)S(1)}) %tuple.49, (s32[]{:T(128)}, s32[]{:T(128)}, s32[]{:T(128)}, ...), branch_computations={%region_1.0_spmd, %region_2.4_spmd} | conditional | flops 549459456 | bytes 17711198 | solution.py:86
  240.4 5.7 %conditional.3 = ((f32[1024,2]{0,1:T(2,128)S(1)}, f32[1024,2]{0,1:T(2,128)S(1)}, f32[1024,2,128]{2,0,1:T(8,128)S(1)})) conditional(s32[]{:T(128)} %convert_element_type.21, (f32[1024,2]{0,1:T(2,128)S(1)}, f32[1024,2]{0,1:T(2,128)S(1)}, f32[1024,2,128]{2,0,1:T(8,128)S(1)}) %tuple.49, (s32[]{:T(128)}, s32[]{:T(128)}, s32[]{:T(128)}, ...), branch_computations={%region_1.0_spmd, %region_2.4_spmd} | conditional | flops 549459456 | bytes 17711198 | solution.py:86
  246.2 5.7 %conditional.3 = ((f32[1024,2]{0,1:T(2,128)S(1)}, f32[1024,2]{0,1:T(2,128)S(1)}, f32[1024,2,128]{2,0,1:T(8,128)S(1)})) conditional(s32[]{:T(128)} %convert_element_type.21, (f32[1024,2]{0,1:T(2,128)S(1)}, f32[1024,2]{0,1:T(2,128)S(1)}, f32[1024,2,128]{2,0,1:T(8,128)S(1)}) %tuple.49, (s32[]{:T(128)}, s32[]{:T(128)}, s32[]{:T(128)}, ...), branch_computations={%region_1.0_spmd, %region_2.4_spmd} | conditional | flops 549459456 | bytes 17711198 | solution.py:86
  252.0 5.7 %conditional.3 = ((f32[1024,2]{0,1:T(2,128)S(1)}, f32[1024,2]{0,1:T(2,128)S(1)}, f32[1024,2,128]{2,0,1:T(8,128)S(1)})) conditional(s32[]{:T(128)} %convert_element_type.21, (f32[1024,2]{0,1:T(2,128)S(1)}, f32[1024,2]{0,1:T(2,128)S(1)}, f32[1024,2,128]{2,0,1:T(8,128)S(1)}) %tuple.49, (s32[]{:T(128)}, s32[]{:T(128)}, s32[]{:T(128)}, ...), branch_computations={%region_1.0_spmd, %region_2.4_spmd} | conditional | flops 549459456 | bytes 17711198 | solution.py:86
  257.7 5.7 %conditional.3 = ((f32[1024,2]{0,1:T(2,128)S(1)}, f32[1024,2]{0,1:T(2,128)S(1)}, f32[1024,2,128]{2,0,1:T(8,128)S(1)})) conditional(s32[]{:T(128)} %convert_element_type.21, (f32[1024,2]{0,1:T(2,128)S(1)}, f32[1024,2]{0,1:T(2,128)S(1)}, f32[1024,2,128]{2,0,1:T(8,128)S(1)}) %tuple.49, (s32[]{:T(128)}, s32[]{:T(128)}, s32[]{:T(128)}, ...), branch_computations={%region_1.0_spmd, %region_2.4_spmd} | conditional | flops 549459456 | bytes 17711198 | solution.py:86
  263.5 5.7 %conditional.3 = ((f32[1024,2]{0,1:T(2,128)S(1)}, f32[1024,2]{0,1:T(2,128)S(1)}, f32[1024,2,128]{2,0,1:T(8,128)S(1)})) conditional(s32[]{:T(128)} %convert_element_type.21, (f32[1024,2]{0,1:T(2,128)S(1)}, f32[1024,2]{0,1:T(2,128)S(1)}, f32[1024,2,128]{2,0,1:T(8,128)S(1)}) %tuple.49, (s32[]{:T(128)}, s32[]{:T(128)}, s32[]{:T(128)}, ...), branch_computations={%region_1.0_spmd, %region_2.4_spmd} | conditional | flops 549459456 | bytes 17711198 | solution.py:86
  269.3 5.7 %conditional.3 = ((f32[1024,2]{0,1:T(2,128)S(1)}, f32[1024,2]{0,1:T(2,128)S(1)}, f32[1024,2,128]{2,0,1:T(8,128)S(1)})) conditional(s32[]{:T(128)} %convert_element_type.21, (f32[1024,2]{0,1:T(2,128)S(1)}, f32[1024,2]{0,1:T(2,128)S(1)}, f32[1024,2,128]{2,0,1:T(8,128)S(1)}) %tuple.49, (s32[]{:T(128)}, s32[]{:T(128)}, s32[]{:T(128)}, ...), branch_computations={%region_1.0_spmd, %region_2.4_spmd} | conditional | flops 549459456 | bytes 17711198 | solution.py:86
  275.0 5.7 %conditional.3 = ((f32[1024,2]{0,1:T(2,128)S(1)}, f32[1024,2]{0,1:T(2,128)S(1)}, f32[1024,2,128]{2,0,1:T(8,128)S(1)})) conditional(s32[]{:T(128)} %convert_element_type.21, (f32[1024,2]{0,1:T(2,128)S(1)}, f32[1024,2]{0,1:T(2,128)S(1)}, f32[1024,2,128]{2,0,1:T(8,128)S(1)}) %tuple.49, (s32[]{:T(128)}, s32[]{:T(128)}, s32[]{:T(128)}, ...), branch_computations={%region_1.0_spmd, %region_2.4_spmd} | conditional | flops 549459456 | bytes 17711198 | solution.py:86
  280.8 5.7 %conditional.3 = ((f32[1024,2]{0,1:T(2,128)S(1)}, f32[1024,2]{0,1:T(2,128)S(1)}, f32[1024,2,128]{2,0,1:T(8,128)S(1)})) conditional(s32[]{:T(128)} %convert_element_type.21, (f32[1024,2]{0,1:T(2,128)S(1)}, f32[1024,2]{0,1:T(2,128)S(1)}, f32[1024,2,128]{2,0,1:T(8,128)S(1)}) %tuple.49, (s32[]{:T(128)}, s32[]{:T(128)}, s32[]{:T(128)}, ...), branch_computations={%region_1.0_spmd, %region_2.4_spmd} | conditional | flops 549459456 | bytes 17711198 | solution.py:86
  286.6 5.7 %conditional.3 = ((f32[1024,2]{0,1:T(2,128)S(1)}, f32[1024,2]{0,1:T(2,128)S(1)}, f32[1024,2,128]{2,0,1:T(8,128)S(1)})) conditional(s32[]{:T(128)} %convert_element_type.21, (f32[1024,2]{0,1:T(2,128)S(1)}, f32[1024,2]{0,1:T(2,128)S(1)}, f32[1024,2,128]{2,0,1:T(8,128)S(1)}) %tuple.49, (s32[]{:T(128)}, s32[]{:T(128)}, s32[]{:T(128)}, ...), branch_computations={%region_1.0_spmd, %region_2.4_spmd} | conditional | flops 549459456 | bytes 17711198 | solution.py:86
  292.4 5.7 %conditional.3 = ((f32[1024,2]{0,1:T(2,128)S(1)}, f32[1024,2]{0,1:T(2,128)S(1)}, f32[1024,2,128]{2,0,1:T(8,128)S(1)})) conditional(s32[]{:T(128)} %convert_element_type.21, (f32[1024,2]{0,1:T(2,128)S(1)}, f32[1024,2]{0,1:T(2,128)S(1)}, f32[1024,2,128]{2,0,1:T(8,128)S(1)}) %tuple.49, (s32[]{:T(128)}, s32[]{:T(128)}, s32[]{:T(128)}, ...), branch_computations={%region_1.0_spmd, %region_2.4_spmd} | conditional | flops 549459456 | bytes 17711198 | solution.py:86
  298.1 5.7 %conditional.3 = ((f32[1024,2]{0,1:T(2,128)S(1)}, f32[1024,2]{0,1:T(2,128)S(1)}, f32[1024,2,128]{2,0,1:T(8,128)S(1)})) conditional(s32[]{:T(128)} %convert_element_type.21, (f32[1024,2]{0,1:T(2,128)S(1)}, f32[1024,2]{0,1:T(2,128)S(1)}, f32[1024,2,128]{2,0,1:T(8,128)S(1)}) %tuple.49, (s32[]{:T(128)}, s32[]{:T(128)}, s32[]{:T(128)}, ...), branch_computations={%region_1.0_spmd, %region_2.4_spmd} | conditional | flops 549459456 | bytes 17711198 | solution.py:86
  303.9 5.7 %conditional.3 = ((f32[1024,2]{0,1:T(2,128)S(1)}, f32[1024,2]{0,1:T(2,128)S(1)}, f32[1024,2,128]{2,0,1:T(8,128)S(1)})) conditional(s32[]{:T(128)} %convert_element_type.21, (f32[1024,2]{0,1:T(2,128)S(1)}, f32[1024,2]{0,1:T(2,128)S(1)}, f32[1024,2,128]{2,0,1:T(8,128)S(1)}) %tuple.49, (s32[]{:T(128)}, s32[]{:T(128)}, s32[]{:T(128)}, ...), branch_computations={%region_1.0_spmd, %region_2.4_spmd} | conditional | flops 549459456 | bytes 17711198 | solution.py:86
  309.7 5.7 %conditional.3 = ((f32[1024,2]{0,1:T(2,128)S(1)}, f32[1024,2]{0,1:T(2,128)S(1)}, f32[1024,2,128]{2,0,1:T(8,128)S(1)})) conditional(s32[]{:T(128)} %convert_element_type.21, (f32[1024,2]{0,1:T(2,128)S(1)}, f32[1024,2]{0,1:T(2,128)S(1)}, f32[1024,2,128]{2,0,1:T(8,128)S(1)}) %tuple.49, (s32[]{:T(128)}, s32[]{:T(128)}, s32[]{:T(128)}, ...), branch_computations={%region_1.0_spmd, %region_2.4_spmd} | conditional | flops 549459456 | bytes 17711198 | solution.py:86
  312.9 2.4 fusion.8
  315.4 5.7 %conditional.3 = ((f32[1024,2]{0,1:T(2,128)S(1)}, f32[1024,2]{0,1:T(2,128)S(1)}, f32[1024,2,128]{2,0,1:T(8,128)S(1)})) conditional(s32[]{:T(128)} %convert_element_type.21, (f32[1024,2]{0,1:T(2,128)S(1)}, f32[1024,2]{0,1:T(2,128)S(1)}, f32[1024,2,128]{2,0,1:T(8,128)S(1)}) %tuple.49, (s32[]{:T(128)}, s32[]{:T(128)}, s32[]{:T(128)}, ...), branch_computations={%region_1.0_spmd, %region_2.4_spmd} | conditional | flops 549459456 | bytes 17711198 | solution.py:86
  318.7 2.4 fusion.8
  321.2 5.7 %conditional.3 = ((f32[1024,2]{0,1:T(2,128)S(1)}, f32[1024,2]{0,1:T(2,128)S(1)}, f32[1024,2,128]{2,0,1:T(8,128)S(1)})) conditional(s32[]{:T(128)} %convert_element_type.21, (f32[1024,2]{0,1:T(2,128)S(1)}, f32[1024,2]{0,1:T(2,128)S(1)}, f32[1024,2,128]{2,0,1:T(8,128)S(1)}) %tuple.49, (s32[]{:T(128)}, s32[]{:T(128)}, s32[]{:T(128)}, ...), branch_computations={%region_1.0_spmd, %region_2.4_spmd} | conditional | flops 549459456 | bytes 17711198 | solution.py:86
  324.5 2.4 fusion.8
  327.0 5.7 %conditional.3 = ((f32[1024,2]{0,1:T(2,128)S(1)}, f32[1024,2]{0,1:T(2,128)S(1)}, f32[1024,2,128]{2,0,1:T(8,128)S(1)})) conditional(s32[]{:T(128)} %convert_element_type.21, (f32[1024,2]{0,1:T(2,128)S(1)}, f32[1024,2]{0,1:T(2,128)S(1)}, f32[1024,2,128]{2,0,1:T(8,128)S(1)}) %tuple.49, (s32[]{:T(128)}, s32[]{:T(128)}, s32[]{:T(128)}, ...), branch_computations={%region_1.0_spmd, %region_2.4_spmd} | conditional | flops 549459456 | bytes 17711198 | solution.py:86
  332.7 5.7 %conditional.3 = ((f32[1024,2]{0,1:T(2,128)S(1)}, f32[1024,2]{0,1:T(2,128)S(1)}, f32[1024,2,128]{2,0,1:T(8,128)S(1)})) conditional(s32[]{:T(128)} %convert_element_type.21, (f32[1024,2]{0,1:T(2,128)S(1)}, f32[1024,2]{0,1:T(2,128)S(1)}, f32[1024,2,128]{2,0,1:T(8,128)S(1)}) %tuple.49, (s32[]{:T(128)}, s32[]{:T(128)}, s32[]{:T(128)}, ...), branch_computations={%region_1.0_spmd, %region_2.4_spmd} | conditional | flops 549459456 | bytes 17711198 | solution.py:86
  338.5 5.7 %conditional.3 = ((f32[1024,2]{0,1:T(2,128)S(1)}, f32[1024,2]{0,1:T(2,128)S(1)}, f32[1024,2,128]{2,0,1:T(8,128)S(1)})) conditional(s32[]{:T(128)} %convert_element_type.21, (f32[1024,2]{0,1:T(2,128)S(1)}, f32[1024,2]{0,1:T(2,128)S(1)}, f32[1024,2,128]{2,0,1:T(8,128)S(1)}) %tuple.49, (s32[]{:T(128)}, s32[]{:T(128)}, s32[]{:T(128)}, ...), branch_computations={%region_1.0_spmd, %region_2.4_spmd} | conditional | flops 549459456 | bytes 17711198 | solution.py:86
  346.6 15.9 %all_to_all.49 = bf16[16,2,8192]{2,1,0:T(2,128)(2,1)S(1)} all-to-all(bf16[16,2,8192]{2,1,0:T(2,128)(2,1)S(1)} %reshape.80), channel_id=1, replica_groups=mesh['seq'=16,'head'=16] {'head'}, dimensions={0} | all-to-all | bytes 1048576 | tf_op jit(solution)/shard_map/all_to_all | solution.py:92
  (339 shorter events, 166.7 us)
Async XLA Ops:
  6.5 0.8 copy-start
  6.5 18.1 %copy-start.1 = (bf16[64,4096]{1,0:T(8,128)(2,1)S(1)}, bf16[64,4096]{1,0:T(8,128)(2,1)}, u32[]{:S(2)}) copy-start(bf16[64,4096]{1,0:T(8,128)(2,1)} %param.7) | copy-start | bytes 1572868
  6.5 147.3 %all-gather.2.cloned.1.call-start = ((), (), s32[]{:S(2)}) async-start(), calls=%async_computation.3 | async-start | bytes 8912896 | tf_op jit(solution)/shard_map/all_gather | solution.py:32
  25.5 14.5 %all-to-all-start.1 = ((bf16[64,16,256]{2,0,1:T(8,128)(2,1)}), bf16[64,16,256]{2,0,1:T(8,128)(2,1)S(1)}, u32[]{:S(2)}, u32[]{:S(2)}) async-start(bf16[64,16,256]{2,0,1:T(8,128)(2,1)} %bitcast.61), calls=%async_computation.1 | async-start | bytes 1048576 | tf_op jit(solution)/shard_map/all_to_all | solution.py:43
Sparse Core Ops, SparseCore 0:
  24.7 129.0 all-gather.1
where the time goes:
time: 373 us; the launch traced here: 371 us
  matrix products  137 us (37%)
  waiting for transfers between devices  123 us (33%)
  other arithmetic  46 us (12%)
  blocking collectives  31.2 us (8%)
  between operations  13.5 us (4%)
  local copies, waits for them, and re-layouts  11.4 us (3%)
  starting transfers between devices  4.94 us (1%)
    all_gather x1, waiting for transfers between devices, in_one_piece(): lax.all_gather(both, axis, axis=dim, tiled=True)  114 us
    dot_general x32, matrix products, work(): jnp.einsum('ghk,kd->ghd', expo.astype(jnp.bfloat16), v_blk, preferred_ele...  77.8 us
    dot_general x32, matrix products, work(): jnp.einsum('ghd,kd->ghk', mine, k_blk, preferred_element_type=jnp.float32)  58.9 us
    reduce_sum x32, other arithmetic, work(): total = factor * total + jnp.sum(expo, axis=2)  31.2 us
    all_to_all x1, blocking collectives, per_device(): lax.all_to_all(output, 'head', split_axis=0, concat_axis=1, tiled=True)  15.9 us
    all_to_all x1, blocking collectives, sent_together(): lax.all_to_all(both, axis, split_axis=split_dim, concat_axis=concat_dim,...  15.3 us
    le x32, other arithmetic, work(): key_pos[None, None, :] <= query_pos[:, None, None]  11.5 us
    all_to_all x1, waiting for transfers between devices, per_device(): lax.all_to_all(arranged, 'head', split_axis=1, concat_axis=0, tiled=True)  9.53 us
  transfers between devices with their start and end apart: 2, of which 2 were waited for; matrix products, arithmetic and copies ran while one was open for 0% of the time, Pallas kernels for 0%

commit v1 on v0

v1 whole, which is shorter than its diff:
```python
import functools
import math

import jax
import jax.numpy as jnp
from jax import lax
from jax.experimental import pallas as pl
from jax.experimental.pallas import tpu as pltpu
from jax.sharding import PartitionSpec as P

H = 32
KV = 4
DH = 128
NX, NY, NZ, NC = 4, 4, 8, 2
TOK = 64
REP = H // KV
COLS = REP * DH
NQ = REP * TOK
CHUNK = NX * NC * 2 * TOK
LOGICAL = pl.DeviceIdType.MESH
NEG = -1e30
FACTOR = math.log2(math.e) / math.sqrt(DH)


def device(x, y, z, c):
    return ((y // 2) * NZ + z, (y % 2) * (NX * NC) + x * NC + c)


def kernel(
    q_hbm, k_hbm, v_hbm, out_hbm,
    kbuf, vbuf, vloc, qin, qt, m_ref, l_ref, o_ref, s_ref, obuf,
    send0, recv0k, recv0v, sendq, recvq,
    sendx, recvx, sendz, recvz, sendd, recvd, sendo, recvo, local_sem,
):
    seq, head = lax.axis_index("seq"), lax.axis_index("head")
    yh, z = seq // NZ, seq % NZ
    yl, x, c = head // (NX * NC), (head % (NX * NC)) // NC, head % NC
    y = yh * 2 + yl
    mirror = NZ - 1 - z
    partner = device(x, y, z, 1 - c)
    bufs = (kbuf, vbuf)

    def remote(src, dst, send, recv, dev):
        return pltpu.make_async_remote_copy(
            src_ref=src, dst_ref=dst, send_sem=send, recv_sem=recv,
            device_id=dev, device_id_type=LOGICAL,
        )

    barrier = pltpu.get_barrier_semaphore()
    peers = [device(x, (y + d) % NY, z, c) for d in (1, 2, 3)]
    peers += [device(x, (y + d) % NY, mirror, c) for d in range(NY)]
    peers += [device((x + d) % NX, y, z, c) for d in (1, 2, 3)]
    peers += [device(x, y, (z + d) % NZ, c) for d in (1, NZ - 1)]
    peers += [partner]
    for dev in peers:
        pl.semaphore_signal(barrier, inc=1, device_id=dev, device_id_type=LOGICAL)
    pl.semaphore_wait(barrier, len(peers))

    def kv_slice(ref, g):
        return ref.at[:, pl.ds(pl.multiple_of(g * DH, DH), DH)]

    rows = pl.ds(pl.multiple_of(yl * TOK, TOK), TOK)
    first = []
    for d in (1, 3, 2):
        g = (y + d) % NY
        dev = device(x, g, z, c)
        ck = remote(kv_slice(k_hbm, g), kbuf.at[z, c, yh, x, rows], send0.at[0, d], recv0k.at[d], dev)
        cv = remote(kv_slice(v_hbm, g), vloc.at[yh, rows], send0.at[1, d], recv0v.at[d], dev)
        ck.start()
        cv.start()
        first += [(ck, cv)]
    lk = pltpu.make_async_copy(kv_slice(k_hbm, y), kbuf.at[z, c, yh, x, rows], local_sem.at[0])
    lv = pltpu.make_async_copy(kv_slice(v_hbm, y), vloc.at[yh, rows], local_sem.at[1])
    lk.start()
    lv.start()

    def q_slice(ref, g):
        return ref.at[:, pl.ds(pl.multiple_of(g * COLS, COLS), COLS)]

    zd = jnp.where(yh == 0, z, mirror)
    q_copies = [
        remote(q_slice(q_hbm, (y + d) % NY), qin.at[y], sendq.at[d], recvq.at[y], device(x, (y + d) % NY, zd, c))
        for d in range(NY)
    ]
    q_own = pltpu.make_async_copy(q_slice(q_hbm, y), qin.at[y], local_sem.at[2])
    for d in (1, 2, 3):
        q_copies[d].start()

    @pl.when(yh == 1)
    def _():
        q_copies[0].start()

    @pl.when(yh == 0)
    def _():
        q_own.start()

    lk.wait()
    for ck, _ in first:
        ck.wait_recv()
    xs = {}
    for a in (0, 1):
        if a == 1:
            lv.wait()
            for _, cv in first:
                cv.wait_recv()
            for h in (0, 1):
                vbuf[z, c, h, x] = vloc[h].astype(jnp.float32).T.astype(jnp.bfloat16)
        for d in (1, 3, 2):
            part = bufs[a].at[z, c, :, x]
            xs[a, d] = remote(part, part, sendx.at[a, d], recvx.at[a, d], device((x + d) % NX, y, z, c))
            xs[a, d].start()

    for p in range(NY):
        @pl.when(y == p)
        def _(p=p):
            @pl.when(yh == 0)
            def _():
                q_own.wait()

        @pl.when((y != p) | (yh == 1))
        def _(p=p):
            remote(qin.at[p], qin.at[p], sendq.at[0], recvq.at[p], partner).wait_recv()

        stacked = jnp.concatenate([qin[p, :, h * DH:(h + 1) * DH] for h in range(REP)], axis=0)
        scaled = (stacked.astype(jnp.float32) * FACTOR).T
        high = scaled.astype(jnp.bfloat16)
        qt[p, :DH] = high
        qt[p, DH:] = (scaled - high.astype(jnp.float32)).astype(jnp.bfloat16)
    m_ref[...] = jnp.full(m_ref.shape, NEG, jnp.float32)
    l_ref[...] = jnp.zeros(l_ref.shape, jnp.float32)
    o_ref[...] = jnp.zeros(o_ref.shape, jnp.float32)

    right, left = device(x, y, (z + 1) % NZ, c), device(x, y, (z + NZ - 1) % NZ, c)
    started = []

    def hop(a, zz, step, way):
        part = bufs[a].at[zz, c]
        cp = remote(part, part, sendz.at[a, way, step], recvz.at[a, way, step], right if way == 0 else left)
        cp.start()
        started.append(cp)

    def arrived(a, zz, step, way):
        part = bufs[a].at[zz, c]
        remote(part, part, sendz.at[a, way, step], recvz.at[a, way, step], partner).wait_recv()

    def across(a, zz, slot):
        part = bufs[a].at[zz, c]
        cp = remote(part, part, sendd.at[a, slot], recvd.at[a, slot], partner)
        cp.start()
        started.append(cp)

    def crossed(a, zz, slot):
        part = bufs[a].at[zz, 1 - c]
        remote(part, part, sendd.at[a, slot], recvd.at[a, slot], partner).wait_recv()

    def count(zz):
        return 1 + (zz <= z).astype(jnp.int32) + (zz <= mirror).astype(jnp.int32)

    def decode(j, zs):
        n1 = count(zs[0])
        second = (j >= n1).astype(jnp.int32)
        zz = zs[0] + second * (zs[-1] - zs[0])
        jj = j - second * n1
        has_early = (zz <= z).astype(jnp.int32)
        is_early = jnp.where(jj == 1, has_early, 0)
        is_late = jnp.where(jj == 0, 0, 1 - is_early)
        diag = is_early * (zz == z).astype(jnp.int32) + is_late * (zz == mirror).astype(jnp.int32)
        return zz, is_late, 1 - is_early, diag

    def chunk_keys(zz, half):
        k = jnp.concatenate([kbuf[zz, cc, half, xx] for cc in range(NC) for xx in range(NX)], axis=0)
        return jnp.concatenate([k, k], axis=1)

    def chunk_values(zz, half):
        return jnp.concatenate([vbuf[zz, cc, half, xx] for cc in range(NC) for xx in range(NX)], axis=1)

    def score(work, t):
        zz, half, group, _ = work
        s_ref[t] = jnp.dot(chunk_keys(zz, half), qt[group * 2 + t], preferred_element_type=jnp.float32)

    def accumulate(work, t, masked):
        zz, half, group, _ = work
        p = group * 2 + t
        s = s_ref[t]
        if masked:
            r = lax.broadcasted_iota(jnp.int32, (CHUNK, NQ), 0)
            k_pos = ((r >> 6) & 1) * 512 + ((r >> 7) & 3) * 128 + (r >> 9) * 64 + (r & 63)
            q_pos = t * 512 + x * 128 + c * 64 + (lax.broadcasted_iota(jnp.int32, (CHUNK, NQ), 1) & 63)
            s = jnp.where(k_pos <= q_pos, s, NEG)
        m_old = m_ref[p]
        m_new = jnp.maximum(m_old, jnp.max(s, axis=0, keepdims=True))
        alpha = jnp.exp2(m_old - m_new)
        e = jnp.exp2(s - m_new)
        m_ref[p] = m_new
        l_ref[p] = l_ref[p] * alpha + jnp.sum(e, axis=0, keepdims=True)
        pv = jnp.dot(chunk_values(zz, half), e.astype(jnp.bfloat16), preferred_element_type=jnp.float32)
        o_ref[p] = o_ref[p] * alpha + pv

    def attend(zs):
        total = count(zs[0])
        if len(zs) > 1:
            total = total + count(zs[1])
        score(decode(0, zs), 0)

        def body(j, carry):
            work = decode(j, zs)
            after = decode(jnp.minimum(j + 1, total - 1), zs)

            def run(masked):
                score(work, 1)
                accumulate(work, 0, masked)
                score(after, 0)
                accumulate(work, 1, masked)

            @pl.when(work[3] == 0)
            def _():
                run(False)

            @pl.when(work[3] == 1)
            def _():
                run(True)

            return carry

        lax.fori_loop(0, total, body, 0)

    for a in (0, 1):
        for d in (1, 3, 2):
            xs[a, d].wait_recv()
        for way in (0, 1):
            hop(a, z, 0, way)
        across(a, z, 0)
    for a in (0, 1):
        crossed(a, z, 0)
    attend((z,))
    for k in (1, 2, 3):
        low, high = (z + NZ - k) % NZ, (z + k) % NZ
        for a in (0, 1):
            for way, zz in ((0, low), (1, high)):
                arrived(a, zz, k - 1, way)
                if k < 3 or a == way:
                    hop(a, zz, k, way)
                across(a, zz, 2 * k - 1 + way)
        for a in (0, 1):
            for way, zz in ((0, low), (1, high)):
                crossed(a, zz, 2 * k - 1 + way)
        attend((low, high))
    far = (z + 4) % NZ
    for a in (0, 1):
        arrived(a, far, 3, a)
        across(a, far, 7)
    for a in (0, 1):
        crossed(a, far, 7)
    attend((far,))

    def piece(p):
        zp = z if p < 2 else mirror
        return remote(obuf.at[p], q_slice(out_hbm, y), sendo.at[p], recvo.at[y], device(x, p, zp, c))

    own = pltpu.make_async_copy(obuf.at[y], q_slice(out_hbm, y), local_sem.at[3])
    for p in range(NY):
        result = (o_ref[p] / l_ref[p]).T.astype(jnp.bfloat16)
        for h in range(REP):
            obuf[p, :, h * DH:(h + 1) * DH] = result[h * TOK:(h + 1) * TOK]
        if p < 2:
            @pl.when(y == p)
            def _():
                own.start()

            @pl.when(y != p)
            def _(p=p):
                piece(p).start()
        else:
            piece(p).start()

    for d in range(NY):
        g = (y + d) % NY
        landing = remote(obuf.at[0], q_slice(out_hbm, g), sendo.at[0], recvo.at[g], partner)
        if d:
            landing.wait_recv()
        else:
            @pl.when(yh == 1)
            def _():
                landing.wait_recv()

            @pl.when(yh == 0)
            def _():
                own.wait()

    for ck, cv in first:
        ck.wait_send()
        cv.wait_send()
    for d in (1, 2, 3):
        q_copies[d].wait_send()
        for a in (0, 1):
            xs[a, d].wait_send()

    @pl.when(yh == 1)
    def _():
        q_copies[0].wait_send()

    for cp in started:
        cp.wait_send()
    for p in range(NY):
        if p < 2:
            @pl.when(y != p)
            def _(p=p):
                piece(p).wait_send()
        else:
            piece(p).wait_send()


def per_device(queries, keys, values):
    bf16, f32 = jnp.bfloat16, jnp.float32
    dma = pltpu.SemaphoreType.DMA
    return pl.pallas_call(
        kernel,
        out_shape=jax.ShapeDtypeStruct(queries.shape, bf16),
        in_specs=[pl.BlockSpec(memory_space=pltpu.HBM)] * 3,
        out_specs=pl.BlockSpec(memory_space=pltpu.HBM),
        scratch_shapes=[
            pltpu.VMEM((NZ, NC, 2, NX, 2 * TOK, DH), bf16),
            pltpu.VMEM((NZ, NC, 2, NX, DH, 2 * TOK), bf16),
            pltpu.VMEM((2, 2 * TOK, DH), bf16),
            pltpu.VMEM((NY, TOK, COLS), bf16),
            pltpu.VMEM((NY, 2 * DH, NQ), bf16),
            pltpu.VMEM((NY, 1, NQ), f32),
            pltpu.VMEM((NY, 1, NQ), f32),
            pltpu.VMEM((NY, DH, NQ), f32),
            pltpu.VMEM((2, CHUNK, NQ), f32),
            pltpu.VMEM((NY, TOK, COLS), bf16),
            dma((2, 4)), dma((4,)), dma((4,)), dma((4,)), dma((4,)),
            dma((2, 4)), dma((2, 4)), dma((2, 2, 4)), dma((2, 2, 4)),
            dma((2, 8)), dma((2, 8)), dma((4,)), dma((4,)), dma((4,)),
        ],
        compiler_params=pltpu.CompilerParams(
            collective_id=0, has_side_effects=True, vmem_limit_bytes=60 * 2**20
        ),
        name="attention",
    )(queries, keys, values)


def solution(mesh):
    spec = P(("seq", "head"), None)
    return jax.shard_map(
        per_device, mesh=mesh, in_specs=(spec, spec, spec), out_specs=spec, check_vma=False
    )
```

time: 373 us -> 96.9 us (0.26)
  the two profiles are of different devices: /device:TPU:249 before, /device:TPU:24 now
where the time goes in v1:
time: 96.9 us; the launch traced here: 96.8 us
  Pallas kernels  94.9 us (98%)
  local copies, waits for them, and re-layouts  1.87 us (2%)
    pallas_call x1, Pallas kernels, per_device(): pl.pallas_call(kernel, out_shape=jax.ShapeDtypeStruct(queries.shape, bf16...  94.9 us

profile of v1, /device:TPU:24, one launch (start us, length us, event | category | flops | bytes accessed | tf_op | source)
XLA Modules:
  0.0 96.8 jit_solution(10506368364829843694)
XLA Ops:
  0.0 94.9 %attention.1 = bf16[64,4096]{1,0:T(8,128)(2,1)} custom-call(bf16[64,4096]{1,0:T(8,128)(2,1)} %q_hbm.1, bf16[64,512]{1,0:T(8,128)(2,1)} %k_hbm.1, bf16[64,512]{1,0:T(8,128)(2,1)} %v_hbm.1), custom_call_target="tpu_custom_call" | custom-call | tf_op jit(solution)/shard_map/attention/pallas_call | solution.py:316
  94.9 1.9 %copy.5 = bf16[64,4096]{1,0:T(8,128)(2,1)} copy(bf16[64,4096]{1,0:T(8,128)(2,1)} %attention.1) | data formatting | bytes 1048576

commit v2 on v1

v2 whole, which is shorter than its diff:
```python
import functools
import math

import jax
import jax.numpy as jnp
from jax import lax
from jax.experimental import pallas as pl
from jax.experimental.pallas import tpu as pltpu
from jax.sharding import PartitionSpec as P

H = 32
KV = 4
DH = 128
NX, NY, NZ, NC = 4, 4, 8, 2
TOK = 64
REP = H // KV
COLS = REP * DH
NQ = REP * TOK
CHUNK = NX * NC * 2 * TOK
LOGICAL = pl.DeviceIdType.MESH
NEG = -1e30
FACTOR = math.log2(math.e) / math.sqrt(DH)


def device(x, y, z, c):
    return ((y // 2) * NZ + z, (y % 2) * (NX * NC) + x * NC + c)


def kernel(
    q_hbm, k_hbm, v_hbm, out_hbm,
    kbuf, vbuf, vloc, qin, qt, m_ref, l_ref, o_ref, s_ref, obuf,
    send0, recv0k, recv0v, sendq, recvq, sendkx, recvkx, sendvx, recvvx,
    sendz, recvz, sendd, recvd, sendo, recvo, local_sem,
):
    seq, head = lax.axis_index("seq"), lax.axis_index("head")
    yh, z = seq // NZ, seq % NZ
    yl, x, c = head // (NX * NC), (head % (NX * NC)) // NC, head % NC
    y = yh * 2 + yl
    partner = device(x, y, z, 1 - c)
    right, left = device(x, y, (z + 1) % NZ, c), device(x, y, (z + NZ - 1) % NZ, c)
    low = [(z + NZ - k) % NZ for k in range(4)]
    high = [(z + k) % NZ for k in range(5)]
    far = high[4]
    started = []

    def remote(src, dst, send, recv, dev):
        return pltpu.make_async_remote_copy(
            src_ref=src, dst_ref=dst, send_sem=send, recv_sem=recv,
            device_id=dev, device_id_type=LOGICAL,
        )

    barrier = pltpu.get_barrier_semaphore()
    peers = [device(x, (y + d) % NY, z, c) for d in (1, 2, 3)]
    peers += [device((x + d) % NX, y, z, c) for d in (1, 2, 3)]
    peers += [right, left, partner]
    for dev in peers:
        pl.semaphore_signal(barrier, inc=1, device_id=dev, device_id_type=LOGICAL)
    pl.semaphore_wait(barrier, len(peers))

    def kv_slice(ref, g):
        return ref.at[:, pl.ds(pl.multiple_of(g * DH, DH), DH)]

    rows = pl.ds(pl.multiple_of(yl * TOK, TOK), TOK)
    first_k, first_v = [], []
    for d in (1, 3, 2):
        g = (y + d) % NY
        dev = device(x, g, z, c)
        first_v.append(remote(kv_slice(v_hbm, g), vloc.at[yh, rows], send0.at[1, d], recv0v.at[d], dev))
        first_k.append(remote(kv_slice(k_hbm, g), kbuf.at[z, c, yh, x, rows], send0.at[0, d], recv0k.at[d], dev))
    own_v = pltpu.make_async_copy(kv_slice(v_hbm, y), vloc.at[yh, rows], local_sem.at[1])
    own_k = pltpu.make_async_copy(kv_slice(k_hbm, y), kbuf.at[z, c, yh, x, rows], local_sem.at[0])
    for cp in first_v + [own_v] + first_k + [own_k]:
        cp.start()

    def q_slice(ref, g):
        return ref.at[:, pl.ds(pl.multiple_of(g * COLS, COLS), COLS)]

    q_copies = [
        remote(q_slice(q_hbm, (y + d) % NY), qin.at[y], sendq.at[d], recvq.at[y], device(x, (y + d) % NY, z, c))
        for d in (1, 3, 2)
    ]
    own_q = pltpu.make_async_copy(q_slice(q_hbm, y), qin.at[y], local_sem.at[2])
    for cp in q_copies + [own_q]:
        cp.start()

    def keys_x(d):
        part = kbuf.at[z, c, :, x]
        return remote(part, part, sendkx.at[d], recvkx.at[d], device((x + d) % NX, y, z, c))

    def values_x(zz, slot, d):
        part = vbuf.at[zz, c, :, x]
        return remote(part, part, sendvx.at[slot, d], recvvx.at[slot, d], device((x + d) % NX, y, z, c))

    def along_z(a, zz, step, way):
        if a == 0:
            part = kbuf.at[zz, c] if step < 3 else kbuf.at[zz, c, way]
        else:
            part = vbuf.at[zz, c, :, x] if step < 3 else vbuf.at[zz, c, way, x]
        return remote(part, part, sendz.at[a, way, step], recvz.at[a, way, step], right if way == 0 else left)

    def across(a, zz, core, slot):
        part = (kbuf, vbuf)[a].at[zz, core]
        return remote(part, part, sendd.at[a, slot], recvd.at[a, slot], partner)

    def go(cp):
        cp.start()
        started.append(cp)

    def spread_values(zz, slot):
        for d in (1, 3, 2):
            go(values_x(zz, slot, d))

    def cross_values(zz, slot):
        for d in (1, 3, 2):
            values_x(zz, slot, d).wait_recv()
        go(across(1, zz, c, slot))

    def crossed(zz, slot):
        for a in (0, 1):
            across(a, zz, 1 - c, slot).wait_recv()

    def advance_values(k):
        if k < 4:
            for way, zz in ((0, low[k]), (1, high[k])):
                along_z(1, zz, k - 1, way).wait_recv()
                go(along_z(1, zz, k, way))
                spread_values(zz, 2 * k - 1 + way)
        else:
            for way in (0, 1):
                along_z(1, far, 3, way).wait_recv()
            spread_values(far, 7)

    def advance_keys(k):
        if k < 4:
            for way, zz in ((0, low[k]), (1, high[k])):
                along_z(0, zz, k - 1, way).wait_recv()
                go(along_z(0, zz, k, way))
                go(across(0, zz, c, 2 * k - 1 + way))
        else:
            for way in (0, 1):
                along_z(0, far, 3, way).wait_recv()
            go(across(0, far, c, 7))

    own_v.wait()
    for cp in first_v:
        cp.wait_recv()
    for h in (0, 1):
        vbuf[z, c, h, x] = vloc[h].astype(jnp.float32).T.astype(jnp.bfloat16)
    own_k.wait()
    for cp in first_k:
        cp.wait_recv()
    for d in (1, 3, 2):
        go(keys_x(d))
    for way in (0, 1):
        go(along_z(1, z, 0, way))
    spread_values(z, 0)

    m_ref[...] = jnp.full(m_ref.shape, NEG, jnp.float32)
    l_ref[...] = jnp.zeros(l_ref.shape, jnp.float32)
    o_ref[...] = jnp.zeros(o_ref.shape, jnp.float32)

    for d in (1, 3, 2):
        keys_x(d).wait_recv()
    for way in (0, 1):
        go(along_z(0, z, 0, way))
    go(across(0, z, c, 0))
    advance_values(1)
    cross_values(z, 0)

    for p in range(NY):
        @pl.when(y == p)
        def _():
            own_q.wait()

        @pl.when(y != p)
        def _(p=p):
            remote(qin.at[p], qin.at[p], sendq.at[0], recvq.at[p], partner).wait_recv()

        stacked = jnp.concatenate([qin[p, :, h * DH:(h + 1) * DH] for h in range(REP)], axis=0)
        scaled = (stacked.astype(jnp.float32) * FACTOR).T
        high_part = scaled.astype(jnp.bfloat16)
        qt[p, :DH] = high_part
        qt[p, DH:] = (scaled - high_part.astype(jnp.float32)).astype(jnp.bfloat16)

    def chunk_keys(zz, half):
        k = jnp.concatenate([kbuf[zz, cc, half, xx] for cc in range(NC) for xx in range(NX)], axis=0)
        return jnp.concatenate([k, k], axis=1)

    def chunk_values(zz, half):
        return jnp.concatenate([vbuf[zz, cc, half, xx] for cc in range(NC) for xx in range(NX)], axis=1)

    def score(work, t):
        zz, half, group = work
        s_ref[t] = jnp.dot(chunk_keys(zz, half), qt[group * 2 + t], preferred_element_type=jnp.float32)

    def accumulate(work, t, masked):
        zz, half, group = work
        p = group * 2 + t
        s = s_ref[t]
        if masked:
            r = lax.broadcasted_iota(jnp.int32, (CHUNK, NQ), 0)
            k_pos = ((r >> 6) & 1) * 512 + ((r >> 7) & 3) * 128 + (r >> 9) * 64 + (r & 63)
            q_pos = t * 512 + x * 128 + c * 64 + (lax.broadcasted_iota(jnp.int32, (CHUNK, NQ), 1) & 63)
            s = jnp.where(k_pos <= q_pos, s, NEG)
        m_old = m_ref[p]
        m_new = jnp.maximum(m_old, jnp.max(s, axis=0, keepdims=True))
        alpha = jnp.exp2(m_old - m_new)
        e = jnp.exp2(s - m_new)
        m_ref[p] = m_new
        l_ref[p] = l_ref[p] * alpha + jnp.sum(e, axis=0, keepdims=True)
        pv = jnp.dot(chunk_values(zz, half), e.astype(jnp.bfloat16), preferred_element_type=jnp.float32)
        o_ref[p] = o_ref[p] * alpha + pv

    def run(work, after, masked):
        score(work, 1)
        accumulate(work, 0, masked)
        if after is not None:
            score(after, 0)
        accumulate(work, 1, masked)

    def reaches(zz):
        return (zz <= z).astype(jnp.int32)

    def attend(zs, early=True):
        extra = 2 if early else 1
        n1 = 1 + extra * reaches(zs[0])
        total = n1 + (1 + extra * reaches(zs[1]) if len(zs) > 1 else 0)

        def decode(j):
            second = (j >= n1).astype(jnp.int32)
            zz = zs[0] + second * (zs[-1] - zs[0])
            jj = j - second * n1
            if not early:
                return zz, (jj == 1).astype(jnp.int32), 1
            return zz, (jj == 2).astype(jnp.int32), 1 - (jj == 0).astype(jnp.int32) * reaches(zz)

        score(decode(0), 0)

        def body(j, carry):
            run(decode(j), decode(jnp.minimum(j + 1, total - 1)), False)
            return carry

        lax.fori_loop(0, total, body, 0)

    def give_back(group):
        for t in (0, 1):
            p = group * 2 + t
            result = (o_ref[p] / l_ref[p]).T.astype(jnp.bfloat16)
            for h in range(REP):
                obuf[p, :, h * DH:(h + 1) * DH] = result[h * TOK:(h + 1) * TOK]

            @pl.when(y == p)
            def _(p=p):
                own_out(p).start()

            @pl.when(y != p)
            def _(p=p):
                piece(p).start()

    def own_out(p):
        return pltpu.make_async_copy(obuf.at[p], q_slice(out_hbm, y), local_sem.at[3])

    def piece(p):
        return remote(obuf.at[p], q_slice(out_hbm, y), sendo.at[p], recvo.at[y], device(x, p, z, c))

    crossed(z, 0)
    score((z, 0, 0), 0)
    run((z, 0, 0), (z, 0, 1), True)
    run((z, 0, 1), (z, 1, 1), False)
    run((z, 1, 1), None, True)
    for k in (1, 2, 3):
        advance_values(k + 1)
        advance_keys(k)
        for way, zz in ((0, low[k]), (1, high[k])):
            cross_values(zz, 2 * k - 1 + way)
        for way, zz in ((0, low[k]), (1, high[k])):
            crossed(zz, 2 * k - 1 + way)
        attend((low[k], high[k]))
    advance_keys(4)
    cross_values(far, 7)
    crossed(far, 7)

    @pl.when(far <= z)
    def _():
        score((far, 0, 0), 0)
        run((far, 0, 0), None, False)

    give_back(0)
    attend((far,), early=False)
    give_back(1)

    for p in range(NY):
        @pl.when(y == p)
        def _(p=p):
            own_out(p).wait()

        @pl.when(y != p)
        def _(p=p):
            remote(obuf.at[p], q_slice(out_hbm, p), sendo.at[p], recvo.at[p], partner).wait_recv()
            piece(p).wait_send()

    for cp in first_k + first_v + q_copies + started:
        cp.wait_send()


def per_device(queries, keys, values):
    bf16, f32 = jnp.bfloat16, jnp.float32
    dma = pltpu.SemaphoreType.DMA
    return pl.pallas_call(
        kernel,
        out_shape=jax.ShapeDtypeStruct(queries.shape, bf16),
        in_specs=[pl.BlockSpec(memory_space=pltpu.HBM)] * 3,
        out_specs=pl.BlockSpec(memory_space=pltpu.HBM),
        scratch_shapes=[
            pltpu.VMEM((NZ, NC, 2, NX, 2 * TOK, DH), bf16),
            pltpu.VMEM((NZ, NC, 2, NX, DH, 2 * TOK), bf16),
            pltpu.VMEM((2, 2 * TOK, DH), bf16),
            pltpu.VMEM((NY, TOK, COLS), bf16),
            pltpu.VMEM((NY, 2 * DH, NQ), bf16),
            pltpu.VMEM((NY, 1, NQ), f32),
            pltpu.VMEM((NY, 1, NQ), f32),
            pltpu.VMEM((NY, DH, NQ), f32),
            pltpu.VMEM((2, CHUNK, NQ), f32),
            pltpu.VMEM((NY, TOK, COLS), bf16),
            dma((2, 4)), dma((4,)), dma((4,)), dma((4,)), dma((4,)),
            dma((4,)), dma((4,)), dma((8, 4)), dma((8, 4)),
            dma((2, 2, 4)), dma((2, 2, 4)), dma((2, 8)), dma((2, 8)),
            dma((4,)), dma((4,)), dma((4,)),
        ],
        compiler_params=pltpu.CompilerParams(
            collective_id=0, has_side_effects=True, vmem_limit_bytes=60 * 2**20
        ),
        name="attention",
    )(queries, keys, values)


def solution(mesh):
    spec = P(("seq", "head"), None)
    return jax.shard_map(
        per_device, mesh=mesh, in_specs=(spec, spec, spec), out_specs=spec, check_vma=False
    )
```

time: 96.9 us -> 69.5 us (0.72)
  the two profiles are of different devices: /device:TPU:24 before, /device:TPU:249 now
where the time goes in v2:
time: 69.5 us; the launch traced here: 69.4 us
  Pallas kernels  67.5 us (97%)
  local copies, waits for them, and re-layouts  1.87 us (3%)
    pallas_call x1, Pallas kernels, per_device(): pl.pallas_call(kernel, out_shape=jax.ShapeDtypeStruct(queries.shape, bf16...  67.5 us
    unnamed x1, local copies, waits for them, and re-layouts  1.87 us

profile of v2, /device:TPU:249, one launch (start us, length us, event | category | flops | bytes accessed | tf_op | source)
XLA Modules:
  0.0 69.4 jit_solution(18178247535526439798)
XLA Ops:
  0.0 67.5 %attention.1 = bf16[64,4096]{1,0:T(8,128)(2,1)} custom-call(bf16[64,4096]{1,0:T(8,128)(2,1)} %q_hbm.1, bf16[64,512]{1,0:T(8,128)(2,1)} %k_hbm.1, bf16[64,512]{1,0:T(8,128)(2,1)} %v_hbm.1), custom_call_target="tpu_custom_call" | custom-call | tf_op jit(solution)/shard_map/attention/pallas_call | solution.py:309
  67.5 1.9 %copy.5 = bf16[64,4096]{1,0:T(8,128)(2,1)} copy(bf16[64,4096]{1,0:T(8,128)(2,1)} %attention.1) | data formatting | bytes 1048576

commit v3 on v2

v3 whole, which is shorter than its diff:
```python
import functools
import math

import jax
import jax.numpy as jnp
from jax import lax
from jax.experimental import pallas as pl
from jax.experimental.pallas import tpu as pltpu
from jax.sharding import PartitionSpec as P

H = 32
KV = 4
DH = 128
NX, NY, NZ, NC = 4, 4, 8, 2
TOK = 64
REP = H // KV
COLS = REP * DH
NQ = REP * TOK
CHUNK = NX * NC * 2 * TOK
LOGICAL = pl.DeviceIdType.MESH
NEG = -1e30
FACTOR = math.log2(math.e) / math.sqrt(DH)


def device(x, y, z, c):
    return ((y // 2) * NZ + z, (y % 2) * (NX * NC) + x * NC + c)


def kernel(
    q_hbm, k_hbm, v_hbm, out_hbm,
    kbuf, vbuf, vloc, qin, qt, m_ref, l_ref, o_ref, s_ref, obuf,
    send0, recv0k, recv0v, sendq, recvq, sent, recvkx, recvvx,
    recvkz, recvvz, recvd, sendo, recvo, local_sem,
):
    seq, head = lax.axis_index("seq"), lax.axis_index("head")
    yh, z = seq // NZ, seq % NZ
    yl, x, c = head // (NX * NC), (head % (NX * NC)) // NC, head % NC
    y = yh * 2 + yl
    partner = device(x, y, z, 1 - c)
    right, left = device(x, y, (z + 1) % NZ, c), device(x, y, (z + NZ - 1) % NZ, c)
    low = [(z + NZ - k) % NZ for k in range(4)]
    high = [(z + k) % NZ for k in range(5)]
    far = high[4]

    def remote(src, dst, send, recv, dev):
        return pltpu.make_async_remote_copy(
            src_ref=src, dst_ref=dst, send_sem=send, recv_sem=recv,
            device_id=dev, device_id_type=LOGICAL,
        )

    @jax.named_scope("enter")
    def enter():
        for dev in peers:
            pl.semaphore_signal(barrier, inc=1, device_id=dev, device_id_type=LOGICAL)
        pl.semaphore_wait(barrier, len(peers))

    barrier = pltpu.get_barrier_semaphore()
    peers = [device(x, (y + d) % NY, z, c) for d in (1, 2, 3)]
    peers += [device((x + d) % NX, y, z, c) for d in (1, 2, 3)]
    peers += [right, left, partner]
    enter()

    def kv_slice(ref, g):
        return ref.at[:, pl.ds(pl.multiple_of(g * DH, DH), DH)]

    rows = pl.ds(pl.multiple_of(yl * TOK, TOK), TOK)
    first_k, first_v = [], []
    for d in (1, 3, 2):
        g = (y + d) % NY
        dev = device(x, g, z, c)
        first_v.append(remote(kv_slice(v_hbm, g), vloc.at[yh, rows], send0.at[0], recv0v.at[0], dev))
        first_k.append(remote(kv_slice(k_hbm, g), kbuf.at[z, c, yh, x, rows], send0.at[0], recv0k.at[0], dev))
    own_v = pltpu.make_async_copy(kv_slice(v_hbm, y), vloc.at[yh, rows], local_sem.at[1])
    own_k = pltpu.make_async_copy(kv_slice(k_hbm, y), kbuf.at[z, c, yh, x, rows], local_sem.at[0])
    for cp in first_v + [own_v] + first_k + [own_k]:
        cp.start()

    def q_slice(ref, g):
        return ref.at[:, pl.ds(pl.multiple_of(g * COLS, COLS), COLS)]

    q_copies = [
        remote(q_slice(q_hbm, (y + d) % NY), qin.at[y], sendq.at[0], recvq.at[0], device(x, (y + d) % NY, z, c))
        for d in (1, 3, 2)
    ]
    own_q = pltpu.make_async_copy(q_slice(q_hbm, y), qin.at[y], local_sem.at[2])
    for cp in q_copies + [own_q]:
        cp.start()

    def keys_x(h, d):
        part = kbuf.at[z, c, h, x]
        return remote(part, part, sent.at[3], recvkx.at[h], device((x + d) % NX, y, z, c))

    def keys_z(zz, step, way, h):
        part = kbuf.at[zz, c, h]
        kind = 2 if step < 3 else 3
        return remote(part, part, sent.at[kind], recvkz.at[step, h], right if way == 0 else left)

    def values_z(zz, step, way):
        part = vbuf.at[zz, c, :, x] if step < 3 else vbuf.at[zz, c, way, x]
        kind = 4 if step < 3 else 3
        return remote(part, part, sent.at[kind], recvvz.at[step], right if way == 0 else left)

    def values_x(zz, slot, h, d):
        part = vbuf.at[zz, c, h, x]
        return remote(part, part, sent.at[1], recvvx.at[slot, h], device((x + d) % NX, y, z, c))

    def across(a, zz, core, slot, h):
        part = (kbuf, vbuf)[a].at[zz, core, h]
        return remote(part, part, sent.at[0], recvd.at[(slot + 1) // 2, h], partner)

    def arrive(part, sem):
        remote(part, part, sent.at[0], sem, partner).wait_recv()

    def leave_by(part, sem):
        remote(part, part, sem, recvo.at[0], partner).wait_send()

    three, twelve = kbuf.at[0, 0, 0, 0:3], kbuf.at[0:3, 0, 0]

    def slots(k):
        return ((0, low[k], 2 * k - 1), (1, high[k], 2 * k)) if k < 4 else ((0, far, 7),)

    @jax.named_scope("spread_values")
    def spread_values(zz, slot, h):
        for d in (1, 3, 2):
            values_x(zz, slot, h, d).start()

    @jax.named_scope("cross_values")
    def cross_values(zz, slot, h):
        arrive(three, recvvx.at[slot, h])
        across(1, zz, c, slot, h).start()

    @jax.named_scope("settle")
    def settle(k, h):
        arrive(kbuf.at[0] if 0 < k < 4 else kbuf.at[0, 0], recvd.at[k, h])

    @jax.named_scope("advance_values")
    def advance_values(k):
        arrive(kbuf.at[0, 0, 0] if k < 4 else kbuf.at[0, 0, 0, 0:2], recvvz.at[k - 1])
        for way, zz, _ in slots(k):
            if k < 4:
                values_z(zz, k, way).start()
        for h in (0, 1):
            for _, zz, slot in slots(k):
                spread_values(zz, slot, h)

    @jax.named_scope("advance_keys")
    def advance_keys(k, h):
        arrive(kbuf.at[0, 0] if k < 4 else kbuf.at[0, 0, 0], recvkz.at[k - 1, h])
        for way, zz, slot in slots(k):
            if k < 3 or (k == 3 and way == h):
                keys_z(zz, k, way, h).start()
            across(0, zz, c, slot, h).start()

    with jax.named_scope("first"):
        own_v.wait()
        arrive(kbuf.at[0, 0, 0, 0:3, 0:TOK], recv0v.at[0])
    for h in (0, 1):
        vbuf[z, c, h, x] = vloc[h].astype(jnp.float32).T.astype(jnp.bfloat16)
    own_k.wait()
    arrive(kbuf.at[0, 0, 0, 0:3, 0:TOK], recv0k.at[0])
    for h in (0, 1):
        for d in (1, 3, 2):
            keys_x(h, d).start()
        if h == 0:
            for way in (0, 1):
                values_z(z, 0, way).start()
        spread_values(z, 0, h)

    m_ref[...] = jnp.full(m_ref.shape, NEG, jnp.float32)
    l_ref[...] = jnp.zeros(l_ref.shape, jnp.float32)
    o_ref[...] = jnp.zeros(o_ref.shape, jnp.float32)

    @jax.named_scope("begin")
    def begin(h):
        arrive(three, recvkx.at[h])
        for way in (0, 1):
            keys_z(z, 0, way, h).start()
        across(0, z, c, 0, h).start()

    advance_values(1)
    begin(0)
    cross_values(z, 0, 0)

    with jax.named_scope("queries"):
        own_q.wait()
        arrive(twelve, recvq.at[0])
        for p in range(NY):
            stacked = jnp.concatenate([qin[p, :, h * DH:(h + 1) * DH] for h in range(REP)], axis=0)
            scaled = (stacked.astype(jnp.float32) * FACTOR).T
            high_part = scaled.astype(jnp.bfloat16)
            qt[p, :DH] = high_part
            qt[p, DH:] = (scaled - high_part.astype(jnp.float32)).astype(jnp.bfloat16)

    def chunk_keys(zz, half):
        k = jnp.concatenate([kbuf[zz, cc, half, xx] for cc in range(NC) for xx in range(NX)], axis=0)
        return jnp.concatenate([k, k], axis=1)

    def chunk_values(zz, half):
        return jnp.concatenate([vbuf[zz, cc, half, xx] for cc in range(NC) for xx in range(NX)], axis=1)

    def score(work, t, place=None):
        zz, half, group = work
        s_ref[t if place is None else place] = jnp.dot(chunk_keys(zz, half), qt[group * 2 + t], preferred_element_type=jnp.float32)

    def accumulate(work, t, masked, place=None):
        zz, half, group = work
        p = group * 2 + t
        s = s_ref[t if place is None else place]
        if masked:
            r = lax.broadcasted_iota(jnp.int32, (CHUNK, NQ), 0)
            k_pos = ((r >> 6) & 1) * 512 + ((r >> 7) & 3) * 128 + (r >> 9) * 64 + (r & 63)
            q_pos = t * 512 + x * 128 + c * 64 + (lax.broadcasted_iota(jnp.int32, (CHUNK, NQ), 1) & 63)
            s = jnp.where(k_pos <= q_pos, s, NEG)
        m_old = m_ref[p]
        m_new = jnp.maximum(m_old, jnp.max(s, axis=0, keepdims=True))
        alpha = jnp.exp2(m_old - m_new)
        e = jnp.exp2(s - m_new)
        m_ref[p] = m_new
        wide = jnp.concatenate([chunk_values(zz, half), jnp.ones((16, CHUNK), jnp.bfloat16)], axis=0)
        pv = jnp.dot(wide, e.astype(jnp.bfloat16), preferred_element_type=jnp.float32)
        l_ref[p] = l_ref[p] * alpha + pv[DH:DH + 1]
        o_ref[p] = o_ref[p] * alpha + pv[:DH]

    def run(work, after, masked):
        score(work, 1)
        accumulate(work, 0, masked)
        if after is not None:
            score(after, 0)
        accumulate(work, 1, masked)

    def reaches(zz):
        return (zz <= z).astype(jnp.int32)

    def first_early(zz):
        return zz, 0, 1 - reaches(zz)

    def choose(flag, a, b):
        return tuple(v + flag * (w - v) for v, w in zip(a, b))

    @jax.named_scope("attend_early")
    def attend_early(zz, then, primed):
        total = 1 + reaches(zz)
        if not primed:
            score(first_early(zz), 0)

        def body(j, carry):
            last = (j == total - 1).astype(jnp.int32)
            run((zz, 0, last), choose(last, (zz, 0, 1), then), False)
            return carry

        lax.fori_loop(0, total, body, 0)

    @jax.named_scope("attend_late")
    def attend_late(a, b):
        total = reaches(a) + reaches(b)

        def body(j, carry):
            second = jnp.maximum(j, 1 - reaches(a))
            run((a + second * (b - a), 1, 1), (b, 1, 1), False)
            return carry

        lax.fori_loop(0, total, body, 0)

    @jax.named_scope("give_back")
    def give_back(p):
        result = (o_ref[p] / l_ref[p]).T.astype(jnp.bfloat16)
        for h in range(REP):
            obuf[p, :, h * DH:(h + 1) * DH] = result[h * TOK:(h + 1) * TOK]

        @pl.when(y == p)
        def _():
            own_out(p).start()

        @pl.when(y != p)
        def _():
            piece(p).start()

    def own_out(p):
        return pltpu.make_async_copy(obuf.at[p], q_slice(out_hbm, y), local_sem.at[3])

    def piece(p):
        return remote(obuf.at[p], q_slice(out_hbm, y), sendo.at[0], recvo.at[0], device(x, p, z, c))

    def cross_all(k, h):
        for _, zz, slot in slots(k):
            cross_values(zz, slot, h)

    settle(0, 0)
    with jax.named_scope("attend_own"):
        score((z, 0, 0), 0)
        run((z, 0, 0), (z, 0, 1), True)
    advance_values(2)
    begin(1)
    cross_values(z, 0, 1)
    with jax.named_scope("attend_own"):
        run((z, 0, 1), None, False)
    advance_keys(1, 0)
    settle(0, 1)
    with jax.named_scope("attend_own"):
        score((z, 1, 1), 0)
        run((z, 1, 1), None, True)
    cross_all(1, 0)
    advance_values(3)
    for k in (1, 2, 3):
        settle(k, 0)
        attend_early(low[k], first_early(high[k]), False)
        if k == 1:
            advance_keys(1, 1)
            cross_all(1, 1)
        else:
            advance_keys(k + 1, 0)
            cross_all(k + 1, 0)
            settle(k, 1)
        start_late = choose(reaches(low[k]), (high[k], 1, 1), (low[k], 1, 1))
        attend_early(high[k], (z, 1, 1) if k == 1 else start_late, True)
        if k == 1:
            advance_values(4)
            advance_keys(2, 0)
            cross_all(2, 0)
            settle(1, 1)
            score(start_late, 0)
        else:
            advance_keys(k + 1, 1)
            cross_all(k + 1, 1)
        if k < 3:
            attend_late(low[k], high[k])
        if k == 1:
            advance_keys(2, 1)
            cross_all(2, 1)
    odd = y % 2
    order = (1 - odd, odd, 3 - odd, 2 + odd)

    def steps(sequence):
        def item(n):
            zz, half, p = sequence[n]
            return (zz, half, p // 2), order[p] - 2 * (p // 2)

        def place(n):
            return n % 2

        for n in range(len(sequence) + 1):
            if n < len(sequence):
                work, t = item(n)
                score(work, t, place(n))
            if n > 0:
                work, t = item(n - 1)
                accumulate(work, t, False, place(n - 1))
                p = sequence[n - 1][2]
                if all(p != q for _, _, q in sequence[n:]):
                    give_back(order[p])

    full = z >= NZ - 3

    @pl.when(full)
    def _():
        settle(4, 0)
        settle(4, 1)
        rest = ((low[3], 1), (high[3], 1), (far, 0), (far, 1))
        steps([(far, 0, 0), (far, 0, 1)] + [(zz, half, p) for p in (2, 3) for zz, half in rest])

    @pl.when(jnp.logical_not(full))
    def _():
        attend_late(low[3], high[3])
        settle(4, 0)
        settle(4, 1)

        @pl.when(far <= z)
        def _():
            steps([(far, 0, 0), (far, 0, 1), (far, 0, 2), (far, 1, 2), (far, 0, 3), (far, 1, 3)])

        @pl.when(far > z)
        def _():
            give_back(order[0])
            give_back(order[1])
            steps([(far, 0, 2), (far, 0, 3)])

    with jax.named_scope("drain"):
        for kind, part in enumerate((kbuf, kbuf.at[0:3], kbuf.at[0:3], kbuf.at[0], twelve)):
            leave_by(part, sent.at[kind])
        leave_by(three, send0.at[0])
        leave_by(twelve, sendq.at[0])

    @jax.named_scope("leave")
    def leave():
        own_out(y).wait()
        arrive(twelve, recvo.at[0])
        leave_by(twelve, sendo.at[0])

    leave()


def per_device(queries, keys, values):
    bf16, f32 = jnp.bfloat16, jnp.float32
    dma = pltpu.SemaphoreType.DMA
    return pl.pallas_call(
        kernel,
        out_shape=jax.ShapeDtypeStruct(queries.shape, bf16),
        in_specs=[pl.BlockSpec(memory_space=pltpu.HBM)] * 3,
        out_specs=pl.BlockSpec(memory_space=pltpu.HBM),
        scratch_shapes=[
            pltpu.VMEM((NZ, NC, 2, NX, 2 * TOK, DH), bf16),
            pltpu.VMEM((NZ, NC, 2, NX, DH, 2 * TOK), bf16),
            pltpu.VMEM((2, 2 * TOK, DH), bf16),
            pltpu.VMEM((NY, TOK, COLS), bf16),
            pltpu.VMEM((NY, 2 * DH, NQ), bf16),
            pltpu.VMEM((NY, 1, NQ), f32),
            pltpu.VMEM((NY, 1, NQ), f32),
            pltpu.VMEM((NY, DH, NQ), f32),
            pltpu.VMEM((2, CHUNK, NQ), f32),
            pltpu.VMEM((NY, TOK, COLS), bf16),
            dma((1,)), dma((1,)), dma((1,)), dma((1,)), dma((1,)),
            dma((5,)), dma((2,)), dma((8, 2)), dma((4, 2)), dma((4,)), dma((5, 2)),
            dma((1,)), dma((1,)), dma((4,)),
        ],
        compiler_params=pltpu.CompilerParams(
            collective_id=0, has_side_effects=True, vmem_limit_bytes=60 * 2**20
        ),
        name="attention",
    )(queries, keys, values)


def solution(mesh):
    spec = P(("seq", "head"), None)
    return jax.shard_map(
        per_device, mesh=mesh, in_specs=(spec, spec, spec), out_specs=spec, check_vma=False
    )
```

time: 69.5 us -> 59 us (0.85)
  Pallas kernels: 67.5 us -> 57 us
    pallas_call x1, Pallas kernels: 67.5 us -> 57 us  [per_device(): pl.pallas_call(kernel, out_shape=jax.ShapeDtypeStruct(queries.shape, bf16...]
where the time goes in v3:
time: 59 us; the launch traced here: 58.9 us
  Pallas kernels  57 us (97%)
  local copies, waits for them, and re-layouts  1.87 us (3%)
    pallas_call x1, Pallas kernels, per_device(): pl.pallas_call(kernel, out_shape=jax.ShapeDtypeStruct(queries.shape, bf16...  57 us
    unnamed x1, local copies, waits for them, and re-layouts  1.87 us

profile of v3, /device:TPU:249, one launch (start us, length us, event | category | flops | bytes accessed | tf_op | source)
XLA Modules:
  0.0 58.9 jit_solution(13837675652751054281)
XLA Ops:
  0.0 57.0 %attention.1 = bf16[64,4096]{1,0:T(8,128)(2,1)} custom-call(bf16[64,4096]{1,0:T(8,128)(2,1)} %q_hbm.1, bf16[64,512]{1,0:T(8,128)(2,1)} %k_hbm.1, bf16[64,512]{1,0:T(8,128)(2,1)} %v_hbm.1), custom_call_target="tpu_custom_call" | custom-call | tf_op jit(solution)/shard_map/attention/pallas_call | solution.py:395
  57.0 1.9 %copy.5 = bf16[64,4096]{1,0:T(8,128)(2,1)} copy(bf16[64,4096]{1,0:T(8,128)(2,1)} %attention.1) | data formatting | bytes 1048576

commit v4 on v3

--- a/solution.py
+++ b/solution.py
@@ -134,11 +134,13 @@
         arrive(kbuf.at[0] if 0 < k < 4 else kbuf.at[0, 0], recvd.at[k, h])
 
     @jax.named_scope("advance_values")
-    def advance_values(k):
+    def advance_values(k, between=None):
         arrive(kbuf.at[0, 0, 0] if k < 4 else kbuf.at[0, 0, 0, 0:2], recvvz.at[k - 1])
         for way, zz, _ in slots(k):
             if k < 4:
                 values_z(zz, k, way).start()
+        if between is not None:
+            between(1)
         for h in (0, 1):
             for _, zz, slot in slots(k):
                 spread_values(zz, slot, h)
@@ -158,13 +160,14 @@
         vbuf[z, c, h, x] = vloc[h].astype(jnp.float32).T.astype(jnp.bfloat16)
     own_k.wait()
     arrive(kbuf.at[0, 0, 0, 0:3, 0:TOK], recv0k.at[0])
-    for h in (0, 1):
+    def begin_x(h):
         for d in (1, 3, 2):
             keys_x(h, d).start()
-        if h == 0:
-            for way in (0, 1):
-                values_z(z, 0, way).start()
         spread_values(z, 0, h)
+
+    for way in (0, 1):
+        values_z(z, 0, way).start()
+    begin_x(0)
 
     m_ref[...] = jnp.full(m_ref.shape, NEG, jnp.float32)
     l_ref[...] = jnp.zeros(l_ref.shape, jnp.float32)
@@ -177,7 +180,7 @@
             keys_z(z, 0, way, h).start()
         across(0, z, c, 0, h).start()
 
-    advance_values(1)
+    advance_values(1, begin_x)
     begin(0)
     cross_values(z, 0, 0)
 
@@ -295,11 +298,11 @@
     with jax.named_scope("attend_own"):
         run((z, 0, 1), None, False)
     advance_keys(1, 0)
+    cross_all(1, 0)
     settle(0, 1)
     with jax.named_scope("attend_own"):
         score((z, 1, 1), 0)
         run((z, 1, 1), None, True)
-    cross_all(1, 0)
     advance_values(3)
     for k in (1, 2, 3):
         settle(k, 0)
@@ -354,9 +357,10 @@
     @pl.when(full)
     def _():
         settle(4, 0)
+        steps([(far, 0, 0), (far, 0, 1)])
         settle(4, 1)
         rest = ((low[3], 1), (high[3], 1), (far, 0), (far, 1))
-        steps([(far, 0, 0), (far, 0, 1)] + [(zz, half, p) for p in (2, 3) for zz, half in rest])
+        steps([(zz, half, p) for p in (2, 3) for zz, half in rest])
 
     @pl.when(jnp.logical_not(full))
     def _():

time: 59 us -> 58.1 us (0.985)
  the two profiles are of different devices: /device:TPU:249 before, /device:TPU:1 now
where the time goes in v4:
time: 58.1 us; the launch traced here: 58 us
  Pallas kernels  56.1 us (97%)
  local copies, waits for them, and re-layouts  1.87 us (3%)
    pallas_call x1, Pallas kernels, per_device(): pl.pallas_call(kernel, out_shape=jax.ShapeDtypeStruct(queries.shape, bf16...  56.1 us
    unnamed x1, local copies, waits for them, and re-layouts  1.87 us

profile of v4, /device:TPU:1, one launch (start us, length us, event | category | flops | bytes accessed | tf_op | source)
XLA Modules:
  0.0 58.0 jit_solution(3532110101388179886)
XLA Ops:
  0.0 56.1 %attention.1 = bf16[64,4096]{1,0:T(8,128)(2,1)} custom-call(bf16[64,4096]{1,0:T(8,128)(2,1)} %q_hbm.1, bf16[64,512]{1,0:T(8,128)(2,1)} %k_hbm.1, bf16[64,512]{1,0:T(8,128)(2,1)} %v_hbm.1), custom_call_target="tpu_custom_call" | custom-call | tf_op jit(solution)/shard_map/attention/pallas_call | solution.py:399
  56.1 1.9 %copy.5 = bf16[64,4096]{1,0:T(8,128)(2,1)} copy(bf16[64,4096]{1,0:T(8,128)(2,1)} %attention.1) | data formatting | bytes 1048576

commit v5 on v4

--- a/solution.py
+++ b/solution.py
@@ -57,7 +57,7 @@
     barrier = pltpu.get_barrier_semaphore()
     peers = [device(x, (y + d) % NY, z, c) for d in (1, 2, 3)]
     peers += [device((x + d) % NX, y, z, c) for d in (1, 2, 3)]
-    peers += [right, left, partner]
+    peers = [right, left] + peers + [partner]
     enter()
 
     def kv_slice(ref, g):
@@ -83,8 +83,6 @@
         for d in (1, 3, 2)
     ]
     own_q = pltpu.make_async_copy(q_slice(q_hbm, y), qin.at[y], local_sem.at[2])
-    for cp in q_copies + [own_q]:
-        cp.start()
 
     def keys_x(h, d):
         part = kbuf.at[z, c, h, x]
@@ -168,6 +166,8 @@
     for way in (0, 1):
         values_z(z, 0, way).start()
     begin_x(0)
+    for cp in q_copies + [own_q]:
+        cp.start()
 
     m_ref[...] = jnp.full(m_ref.shape, NEG, jnp.float32)
     l_ref[...] = jnp.zeros(l_ref.shape, jnp.float32)

time: 58.1 us -> 57.3 us (0.986)
  Pallas kernels: 56.1 us -> 55.2 us
    pallas_call x1, Pallas kernels: 56.1 us -> 55.2 us  [per_device(): pl.pallas_call(kernel, out_shape=jax.ShapeDtypeStruct(queries.shape, bf16...]
where the time goes in v5:
time: 57.3 us; the launch traced here: 57.1 us
  Pallas kernels  55.2 us (96%)
  local copies, waits for them, and re-layouts  1.87 us (3%)
    pallas_call x1, Pallas kernels, per_device(): pl.pallas_call(kernel, out_shape=jax.ShapeDtypeStruct(queries.shape, bf16...  55.2 us
    unnamed x1, local copies, waits for them, and re-layouts  1.87 us

profile of v5, /device:TPU:1, one launch (start us, length us, event | category | flops | bytes accessed | tf_op | source)
XLA Modules:
  0.0 57.1 jit_solution(12715140797639649422)
XLA Ops:
  0.0 55.2 %attention.1 = bf16[64,4096]{1,0:T(8,128)(2,1)} custom-call(bf16[64,4096]{1,0:T(8,128)(2,1)} %q_hbm.1, bf16[64,512]{1,0:T(8,128)(2,1)} %k_hbm.1, bf16[64,512]{1,0:T(8,128)(2,1)} %v_hbm.1), custom_call_target="tpu_custom_call" | custom-call | tf_op jit(solution)/shard_map/attention/pallas_call | solution.py:399
  55.2 1.9 %copy.5 = bf16[64,4096]{1,0:T(8,128)(2,1)} copy(bf16[64,4096]{1,0:T(8,128)(2,1)} %attention.1) | data formatting | bytes 1048576
